TPU v7x, 32 devices: a whole 2x2x4 slice. The times are simulated.
32 devices in a mesh: mp: 4 (over y, x), nodes: 8 (over z, core).
Axes of the slice: x: 2, y: 2, z: 4, core: 2. Of those that a mesh axis runs over, the one named last changes fastest.
Arguments:
- grid_latent: float32 [16384, 512], P('nodes'), may hold values from -6 to 6
- mesh_latent: float32 [1024, 512], P('nodes'), may hold values from -250 to 250
- enc_grid_w: float32 [512, 512], P(None, 'mp'), may hold values from -0.25 to 0.25
- enc_mesh_w: float32 [512, 512], P(None, 'mp'), may hold values from -0.25 to 0.25
- enc_out_w: float32 [512, 512], P('mp'), may hold values from -0.25 to 0.25
- block_gain: float32 [512], replicated, may hold values from 0.5 to 1.5
- query_w: float32 [512, 512], P(None, 'mp'), may hold values from -1 to 1
- key_w: float32 [512, 512], P(None, 'mp'), may hold values from -1 to 1
- value_w: float32 [512, 512], P(None, 'mp'), may hold values from -0.25 to 0.25
- out_w: float32 [512, 512], P('mp'), may hold values from -0.25 to 0.25
- up_w: float32 [512, 2048], P(None, 'mp'), may hold values from -0.25 to 0.25
- down_w: float32 [2048, 512], P('mp'), may hold values from -0.125 to 0.125
- dec_gain: float32 [512], replicated, may hold values from 0.5 to 1.5
- dec_grid_w: float32 [512, 512], P(None, 'mp'), may hold values from -0.25 to 0.25
- dec_mesh_w: float32 [512, 512], P(None, 'mp'), may hold values from -0.25 to 0.25
- dec_out_w: float32 [512, 512], P('mp'), may hold values from -0.25 to 0.25
- neighbor_blocks: int32 [8, 16], replicated, may hold values from 0 to 7, as said below
- enc_tiles: int32 [256, 2], P('nodes'), may hold values from -1 to 127, as said below
- enc_edges: int32 [256, 2, 128], P('nodes'), may hold values from 0 to 127
- dec_tiles: int32 [384, 2], P('nodes'), may hold values from 0 to 127, as said below
- dec_edges: int32 [384, 2, 128], P('nodes'), may hold values from 0 to 127
Outputs:
- grid_out: float32 [16384, 512], P('nodes', 'mp')
Inputs may be any that keep to these rules, and one draw needn't show every extreme that they name: `neighbor_blocks`: rows i * 1 to (i + 1) - 1 are the query blocks of index i of nodes; among all entries of those rows, the blocks of any one index j of nodes (ids j * 1 to (j + 1) - 1) are named at most 4 times, and for every i some j is named exactly 4 times. Entries may repeat. `enc_tiles`: tile slots i * 32 to (i + 1) * 32 - 1 belong to index i of nodes; a live tile names a grid block and a mesh block both of index i; an unused slot holds -1 in both columns; on each index the live slots come first, their number differs between indices, and some index has all 32 slots live. `dec_tiles`: tiles i * 48 to (i + 1) * 48 - 1 belong to index i of nodes; each names a grid block of index i and a mesh block of index i - 1, i or i + 1 of nodes (counted around the axis).
All inputs are finite; a program needn't handle non-finite values.
Results may differ from a plain program's by a relative error of at most 0.000098.
Values sent between devices are 32-bit elements; how exact they have to be, the bound alone decides.
No kernel may reach another device: no remote copies, remote signals or barrier semaphores. Data moves between devices by JAX's collectives and lax.ppermute only.
A program may use at most 128 MiB of HBM per device.

v0:
```python
import math
import jax
import jax.numpy as jnp
from jax import lax
from jax.sharding import PartitionSpec as P

HEAD_DIM = 128
NODE_BLOCK = 128
FULL_PRECISION = lax.Precision.HIGHEST


def padded(shard, sides, width):
    for axis, dim in sides:
        devices, length = (lax.axis_size(axis), shard.shape[dim])
        up = [(i, (i + 1) % devices) for i in range(devices)]
        down = [(j, i) for i, j in up]
        last = lax.slice_in_dim(shard, length - width, length, axis=dim)
        initial = lax.slice_in_dim(shard, 0, width, axis=dim)
        before = lax.ppermute(last, axis, up)
        after = lax.ppermute(initial, axis, down)
        shard = jnp.concatenate([before, shard, after], axis=dim)
    return shard


def product(matrix, weight):
    return jnp.dot(matrix, weight, precision=FULL_PRECISION, preferred_element_type=jnp.float32)


def layer_norm(inputs, scales):
    centre = jnp.mean(inputs, axis=-1, keepdims=True)
    shifted = inputs - centre
    spread = jnp.mean(shifted * shifted, axis=-1, keepdims=True)
    return shifted * lax.rsqrt(spread + 1e-05) * scales


def edge_pass(
    source_side, target_side, source_block, target_block, edge_ids, tile_live, target_blocks
):
    source = source_block[:, None] * NODE_BLOCK + edge_ids[:, 0, :]
    target = target_block[:, None] * NODE_BLOCK + edge_ids[:, 1, :]
    message = jax.nn.silu(source_side[source] + target_side[target]) * tile_live[:, None, None]
    within = (edge_ids[:, 1, :][:, None, :] == jnp.arange(NODE_BLOCK)[None, :, None]).astype(
        jnp.float32
    )
    tile_sums = jnp.einsum("tne,teh->tnh", within, message, precision=FULL_PRECISION)
    placing = (target_block[None, :] == jnp.arange(target_blocks)[:, None]).astype(jnp.float32)
    summed = jnp.einsum("bt,tnh->bnh", placing, tile_sums, precision=FULL_PRECISION)
    return summed.reshape(target_blocks * NODE_BLOCK, -1)


def per_device(
    grid_latent,
    mesh_latent,
    enc_grid_w,
    enc_mesh_w,
    enc_out_w,
    block_gain,
    query_w,
    key_w,
    value_w,
    out_w,
    up_w,
    down_w,
    dec_gain,
    dec_grid_w,
    dec_mesh_w,
    dec_out_w,
    neighbor_blocks,
    enc_tiles,
    enc_edges,
    dec_tiles,
    dec_edges,
):
    me_node = lax.axis_index("nodes")
    nodes_count = lax.axis_size("nodes")
    grid_rows = grid_latent.shape[0]
    node_rows = mesh_latent.shape[0]
    grid_blocks = grid_rows // NODE_BLOCK
    node_blocks = node_rows // NODE_BLOCK
    grid_enc = product(grid_latent, enc_grid_w)
    mesh_enc = product(mesh_latent, enc_mesh_w)
    tile_live = enc_tiles[:, 0] >= 0
    source_block = jnp.where(tile_live, enc_tiles[:, 0] - me_node * grid_blocks, 0)
    target_block = jnp.where(tile_live, enc_tiles[:, 1] - me_node * node_blocks, 0)
    enc_agg = edge_pass(
        grid_enc,
        mesh_enc,
        source_block,
        target_block,
        enc_edges,
        tile_live.astype(jnp.float32),
        node_blocks,
    )
    enc_total = lax.psum(product(enc_agg, enc_out_w), "mp")
    mesh_one = mesh_latent + enc_total
    normed = layer_norm(mesh_one, block_gain)
    queries = product(normed, query_w)
    key_rows = product(normed, key_w)
    value_rows = product(normed, value_w)
    head_cols = queries.shape[1]
    heads_here = head_cols // HEAD_DIM
    key_values = jnp.concatenate([key_rows, value_rows], axis=1)
    query_blocks = queries.reshape(node_blocks, NODE_BLOCK, heads_here, HEAD_DIM)
    own_lists = lax.dynamic_slice_in_dim(neighbor_blocks, me_node * node_blocks, node_blocks, 0)
    key_piece = lax.all_gather(key_values, "nodes", axis=0, tiled=True)
    running_max = jnp.full((node_blocks, heads_here, NODE_BLOCK), -1e30, jnp.float32)
    row_count = key_piece.shape[0]
    piece_block = jnp.arange(row_count) // NODE_BLOCK
    repeats = jnp.sum(
        (own_lists[:, :, None] == piece_block[None, None, :]).astype(jnp.float32), axis=1
    )
    near_keys = key_piece[:, :head_cols].reshape(row_count, heads_here, HEAD_DIM)
    near_values = key_piece[:, head_cols:].reshape(row_count, heads_here, HEAD_DIM)
    scores = jnp.einsum(
        "bqhd,khd->bhqk", query_blocks, near_keys, precision=FULL_PRECISION
    ) / math.sqrt(HEAD_DIM)
    scores = jnp.where((repeats > 0)[:, None, None, :], scores, -1e30)
    new_max = jnp.maximum(running_max, jnp.max(scores, axis=-1))
    weights = jnp.exp(scores - new_max[..., None]) * repeats[:, None, None, :]
    running_sum = jnp.sum(weights, axis=-1)
    running_out = jnp.einsum("bhqk,khd->bhqd", weights, near_values, precision=FULL_PRECISION)
    running_max, running_sum, running_out = (new_max, running_sum, running_out)
    attended = (
        (running_out / running_sum[..., None]).transpose(0, 2, 1, 3).reshape(node_rows, head_cols)
    )
    hidden = jax.nn.silu(product(normed, up_w))
    block_total = lax.psum(product(attended, out_w) + product(hidden, down_w), "mp")
    mesh_two = mesh_one + block_total
    mesh_normed = layer_norm(mesh_two, dec_gain)
    all_blocks = node_blocks * nodes_count
    dec_source = (dec_tiles[:, 0] - (me_node - 1) * node_blocks) % all_blocks
    dec_target = dec_tiles[:, 1] - me_node * grid_blocks
    mesh_dec = product(mesh_normed, dec_mesh_w)
    grid_dec = product(grid_latent, dec_grid_w)
    beside_all = padded(mesh_dec, (("nodes", 0),), node_rows)
    every_tile = jnp.ones((dec_tiles.shape[0],), jnp.float32)
    dec_agg = edge_pass(
        beside_all, grid_dec, dec_source, dec_target, dec_edges, every_tile, grid_blocks
    )
    decoded = lax.psum_scatter(product(dec_agg, dec_out_w), "mp", scatter_dimension=1, tiled=True)
    share_cols = decoded.shape[1]
    grid_share = lax.dynamic_slice_in_dim(
        grid_latent, lax.axis_index("mp") * share_cols, share_cols, 1
    )
    return grid_share + decoded


def solution(mesh):
    in_specs = (
        P("nodes", None),
        P("nodes", None),
        P(None, "mp"),
        P(None, "mp"),
        P("mp", None),
        P(),
        P(None, "mp"),
        P(None, "mp"),
        P(None, "mp"),
        P("mp", None),
        P(None, "mp"),
        P("mp", None),
        P(),
        P(None, "mp"),
        P(None, "mp"),
        P("mp", None),
        P(),
        P("nodes", None),
        P("nodes", None, None),
        P("nodes", None),
        P("nodes", None, None),
    )
    out_specs = P("nodes", "mp")
    return jax.shard_map(
        per_device, mesh=mesh, in_specs=in_specs, out_specs=out_specs, check_vma=False
    )
```

profile of v0, /device:TPU:0, one launch (start us, length us, event | category | flops | bytes accessed | tf_op | source)
XLA Modules:
  0.0 294.3 jit_solution(3935935170186829278)
XLA Ops:
  8.9 1.4 fusion.81
  10.4 5.2 %fusion.80 = f32[2048,128]{1,0:T(8,128)S(1)} fusion(f32[2048,512]{1,0:T(8,128)} %param.21, f32[512,128]{1,0:T(8,128)} %param.23), kind=kOutput, calls=%fused_computation.122 | convolution fusion | flops 1610612736 | bytes 5505024 | tf_op jit(solution)/shard_map/dot_general | solution.py:26
  15.7 14.2 %gather_fusion = f32[4096,128]{1,0:T(8,128)} fusion(f32[2048,128]{1,0:T(8,128)S(1)} %fusion.80, s32[4096]{0:T(1024)S(1)} %get-tuple-element.20), kind=kCustom, calls=%fused_computation | custom fusion | bytes 4210688 | tf_op jit(solution)/shard_map/gather | solution.py:41
  29.9 14.2 %gather_fusion.1 = f32[4096,128]{1,0:T(8,128)} fusion(f32[128,128]{1,0:T(8,128)S(1)} %fusion.81, s32[4096]{0:T(1024)S(1)} %get-tuple-element.21), kind=kCustom, calls=%fused_computation.1 | custom fusion | bytes 4210688 | tf_op jit(solution)/shard_map/gather | solution.py:41
  44.0 1.8 add.225
  45.9 1.9 fusion.10
  47.9 2.0 fusion.8
  49.8 1.1 fusion.82
  51.0 45.9 %all-reduce.3.cloned.1.call-done = f32[128,512]{1,0:T(8,128)} async-done(((f32[128,512]{1,0:T(8,128)}), f32[128,512]{1,0:T(8,128)}) %all-reduce.3.cloned.1.call-update) | async-done | bytes 262160 | tf_op jit(solution)/shard_map/psum | solution.py:94
  101.2 5.3 %fusion.83 = f32[2048,128]{1,0:T(8,128)S(1)} fusion(f32[2048,512]{1,0:T(8,128)} %param.21, f32[512,128]{1,0:T(8,128)S(1)} %copy-done.10), kind=kOutput, calls=%fused_computation.125 | convolution fusion | flops 1610612736 | bytes 5505024 | tf_op jit(solution)/shard_map/dot_general | solution.py:26
  108.6 15.6 %all-gather.2.cloned.1.call-done = f32[1024,256]{0,1:T(8,128)} async-done(((f32[128,256]{0,1:T(8,128)}), f32[1024,256]{0,1:T(8,128)}) %all-gather.2.cloned.1.call-update) | async-done | bytes 1048592 | tf_op jit(solution)/shard_map/all_gather | solution.py:105
  124.2 2.1 fusion.78
  126.5 1.8 fusion.22
  128.4 1.1 convolution_add_fusion
  129.7 41.8 %all-reduce.5.cloned.1.call-done = f32[128,512]{1,0:T(8,128)} async-done(((f32[128,512]{1,0:T(8,128)}), f32[128,512]{1,0:T(8,128)}) %all-reduce.5.cloned.1.call-update) | async-done | bytes 262160 | tf_op jit(solution)/shard_map/psum | solution.py:127
  173.2 2.3 collective-permute-start.1
  175.6 21.1 %gather_fusion.3 = f32[6144,128]{1,0:T(8,128)} fusion(f32[2048,128]{1,0:T(8,128)S(1)} %fusion.83, s32[6144]{0:T(1024)S(1)} %get-tuple-element.23), kind=kCustom, calls=%fused_computation.3 | custom fusion | bytes 6316032 | tf_op jit(solution)/shard_map/gather | solution.py:41
  196.7 21.0 %gather_fusion.2 = f32[6144,128]{1,0:T(8,128)} fusion(f32[384,128]{1,0:T(8,128)S(1)} %pad_maximum_fusion, s32[6144]{0:T(1024)S(1)} %get-tuple-element.22), kind=kCustom, calls=%fused_computation.2 | custom fusion | bytes 6316032 | tf_op jit(solution)/shard_map/gather | solution.py:41
  217.8 3.2 %add.226 = f32[6144,128]{1,0:T(8,128)S(1)} add(f32[6144,128]{1,0:T(8,128)} %gather_fusion.2, f32[6144,128]{1,0:T(8,128)} %gather_fusion.3) | non-fusion elementwise | flops 786432 | bytes 9437184 | tf_op jit(solution)/shard_map/add | solution.py:41
  220.9 3.0 %fusion.2 = f32[48,128,128]{2,1,0:T(8,128)S(1)} fusion(f32[48,128,128]{2,1,0:T(8,128)S(1)} %bitcast.94, s32[48,128]{1,0:T(8,128)S(1)} %bitcast.98), kind=kOutput, calls=%fused_computation.6 | convolution fusion | flops 1211891712 | bytes 6316032 | tf_op jit(solution)/shard_map/tne,teh->tnh/dot_general | solution.py:45
  223.9 2.9 fusion
  227.2 4.9 %fusion.84 = f32[2048,512]{1,0:T(8,128)} fusion(f32[2048,128]{1,0:T(8,128)S(1)} %bitcast.93, f32[128,512]{1,0:T(8,128)S(1)} %copy-done.11), kind=kOutput, calls=%fused_computation.126 | convolution fusion | flops 1610612736 | bytes 5505024 | tf_op jit(solution)/shard_map/dot_general | solution.py:26
  232.2 53.0 %reduce-scatter.2.cloned.1.call-done = f32[2048,128]{1,0:T(8,128)} async-done(((f32[2048,512]{1,0:T(8,128)}), f32[2048,128]{1,0:T(8,128)}) %reduce-scatter.2.cloned.1.call-update) | async-done | bytes 1048592 | tf_op jit(solution)/shard_map/reduce_scatter | solution.py:140
  285.1 2.6 dynamic-slice_add_fusion
  (75 shorter events, 11.3 us)
Async XLA Ops:
  6.5 100.5 %copy-start = (f32[512,512]{1,0:T(8,128)S(1)}, f32[512,512]{1,0:T(8,128)}, u32[]{:S(2)}) copy-start(f32[512,512]{1,0:T(8,128)} %param.31) | copy-start | bytes 3145732
  6.5 90.3 %all-reduce.3.cloned.1.call-start = ((), (), s32[]{:S(2)}) async-start(), calls=%async_computation.1 | async-start | bytes 524288 | tf_op jit(solution)/shard_map/psum | solution.py:94
  29.9 14.2 %copy-start.1 = (f32[4096,128]{1,0:T(8,128)S(1)}, f32[4096,128]{1,0:T(8,128)}, u32[]{:S(2)}) copy-start(f32[4096,128]{1,0:T(8,128)} %gather_fusion) | copy-start | bytes 6291460
  45.8 1.9 copy-start.14
  45.9 4.0 %copy-start.4 = (f32[128,512]{1,0:T(8,128)S(1)}, f32[128,512]{1,0:T(8,128)}, u32[]{:S(2)}) copy-start(f32[128,512]{1,0:T(8,128)} %param.25) | copy-start | bytes 786436
  47.8 49.1 %copy-start.3 = (f32[128,512]{1,0:T(8,128)S(1)}, f32[128,512]{1,0:T(8,128)}, u32[]{:S(2)}) copy-start(f32[128,512]{1,0:T(8,128)} %param.22) | copy-start | bytes 786436
  47.8 50.3 %copy-start.5 = (f32[512,128]{1,0:T(8,128)S(1)}, f32[512,128]{1,0:T(8,128)}, u32[]{:S(2)}) copy-start(f32[512,128]{1,0:T(8,128)} %param.29) | copy-start | bytes 786436
  47.8 50.3 %copy-start.13 = (f32[512]{0:T(512)S(1)}, f32[512]{0:T(512)}, u32[]{:S(2)}) copy-start(f32[512]{0:T(512)} %param.26) | copy-start | bytes 6148
  47.8 51.0 %copy-start.6 = (f32[512,128]{1,0:T(8,128)S(1)}, f32[512,128]{1,0:T(8,128)}, u32[]{:S(2)}) copy-start(f32[512,128]{1,0:T(8,128)} %param.28) | copy-start | bytes 786436
  47.8 53.4 %copy-start.10 = (f32[512,128]{1,0:T(8,128)S(1)}, f32[512,128]{1,0:T(8,128)}, u32[]{:S(2)}) copy-start(f32[512,128]{1,0:T(8,128)} %param.34) | copy-start | bytes 786436
  50.9 73.3 %all-gather.2.cloned.1.call-start = ((), (), s32[]{:S(2)}) async-start(), calls=%async_computation.2 | async-start | bytes 1179648 | tf_op jit(solution)/shard_map/all_gather | solution.py:105
  98.8 7.7 %copy-start.7 = (f32[512,128]{1,0:T(8,128)S(1)}, f32[512,128]{1,0:T(8,128)}, u32[]{:S(2)}) copy-start(f32[512,128]{1,0:T(8,128)} %param.27) | copy-start | bytes 786436
  100.2 71.3 %all-reduce.5.cloned.1.call-start = ((), (), s32[]{:S(2)}) async-start(), calls=%async_computation.3 | async-start | bytes 524288 | tf_op jit(solution)/shard_map/psum | solution.py:127
  101.2 6.6 %copy-start.2 = (f32[512,512]{1,0:T(8,128)S(1)}, f32[512,512]{1,0:T(8,128)}, u32[]{:S(2)}) copy-start(f32[512,512]{1,0:T(8,128)} %param.32) | copy-start | bytes 3145732
  106.5 21.8 %copy-start.8 = (f32[128,512]{1,0:T(8,128)S(1)}, f32[128,512]{1,0:T(8,128)}, u32[]{:S(2)}) copy-start(f32[128,512]{1,0:T(8,128)} %param.30) | copy-start | bytes 786436
  107.0 22.6 %copy-start.16 = (s32[48,2]{0,1:T(2,128)S(1)}, s32[48,2]{0,1:T(2,128)}, u32[]{:S(2)}) copy-start(s32[48,2]{0,1:T(2,128)} %param.40) | copy-start | bytes 1156
  107.0 22.6 %copy-start.12 = (s32[48,2,128]{2,1,0:T(2,128)S(1)}, s32[48,2,128]{2,1,0:T(2,128)}, u32[]{:S(2)}) copy-start(s32[48,2,128]{2,1,0:T(2,128)} %param.41) | copy-start | bytes 147460
  107.8 65.0 %copy-start.9 = (f32[512,128]{1,0:T(8,128)S(1)}, f32[512,128]{1,0:T(8,128)}, u32[]{:S(2)}) copy-start(f32[512,128]{1,0:T(8,128)} %param.35) | copy-start | bytes 786436
  107.8 65.0 %copy-start.15 = (f32[512]{0:T(512)S(1)}, f32[512]{0:T(512)}, u32[]{:S(2)}) copy-start(f32[512]{0:T(512)} %param.33) | copy-start | bytes 6148
  129.5 155.6 %reduce-scatter.2.cloned.1.call-start = ((), (), s32[]{:S(2)}) async-start(), calls=%async_computation.4 | async-start | bytes 5242880 | tf_op jit(solution)/shard_map/reduce_scatter | solution.py:140
  173.2 23.5 %collective-permute-start.1 = (f32[128,128]{1,0:T(8,128)S(1)}, f32[128,128]{1,0:T(8,128)S(1)}, u32[]{:S(2)}, u32[]{:S(2)}) collective-permute-start(f32[128,128]{1,0:T(8,128)S(1)} %fusion.31), channel_id=1, source_target_pairs={{1,0},{2,1},{3,2},{4,3},{5,4},{6,5},{7,6},{0,7},{9,8},{10,9},{11,1... | collective-permute-start | bytes 196616 | tf_op jit(solution)/shard_map/ppermute | solution.py:20
  175.6 21.2 %collective-permute-start = (f32[128,128]{1,0:T(8,128)S(1)}, f32[128,128]{1,0:T(8,128)S(1)}, u32[]{:S(2)}, u32[]{:S(2)}) collective-permute-start(f32[128,128]{1,0:T(8,128)S(1)} %fusion.31), channel_id=1, source_target_pairs={{0,1},{1,2},{2,3},{3,4},{4,5},{5,6},{6,7},{7,0},{8,9},{9,10},{10,1... | collective-permute-start | bytes 196616 | tf_op jit(solution)/shard_map/ppermute | solution.py:19
  223.9 3.3 %copy-start.11 = (f32[128,512]{1,0:T(8,128)S(1)}, f32[128,512]{1,0:T(8,128)}, u32[]{:S(2)}) copy-start(f32[128,512]{1,0:T(8,128)} %param.36) | copy-start | bytes 786436
Sparse Core Ops, SparseCore 0:
  51.0 45.7 all-reduce.2
  100.3 23.8 all-gather.1
  129.6 41.7 all-reduce.4
  232.3 52.8 reduce-scatter.1
where the time goes:
time: 295 us; the launch traced here: 294 us
  waiting for transfers between devices  156 us (53%)
  local copies, waits for them, and re-layouts  72.5 us (25%)
  matrix products  36.4 us (12%)
  between operations  13.6 us (5%)
  other arithmetic  12.8 us (4%)
    reduce_scatter x1, waiting for transfers between devices, per_device(): lax.psum_scatter(product(dec_agg, dec_out_w), 'mp', scatter_dimension=1,...  53 us
    psum x1, waiting for transfers between devices, per_device(): enc_total = lax.psum(product(enc_agg, enc_out_w), 'mp')  45.9 us
    psum x1, waiting for transfers between devices, per_device(): lax.psum(product(attended, out_w) + product(hidden, down_w), 'mp')  41.8 us
    gather x2, local copies, waits for them, and re-layouts, edge_pass(): target_side[target]  35.2 us
    gather x2, local copies, waits for them, and re-layouts, edge_pass(): source_side[source] + target_side[target]  35.2 us
    dot_general x12, matrix products, product(): jnp.dot(matrix, weight, precision=FULL_PRECISION, preferred_element_type=...  22.7 us
    all_gather x1, waiting for transfers between devices, per_device(): key_piece = lax.all_gather(key_values, 'nodes', axis=0, tiled=True)  15.6 us
  transfers between devices with their start and end apart: 6, of which 4 were waited for; matrix products, arithmetic and copies ran while one was open for 10% of the time, Pallas kernels for 0%

commit v1 on v0

--- a/solution.py
+++ b/solution.py
@@ -91,7 +91,7 @@
         tile_live.astype(jnp.float32),
         node_blocks,
     )
-    enc_total = lax.psum(product(enc_agg, enc_out_w), "mp")
+    enc_total = jnp.sum(lax.all_gather(product(enc_agg, enc_out_w), "mp"), axis=0)
     mesh_one = mesh_latent + enc_total
     normed = layer_norm(mesh_one, block_gain)
     queries = product(normed, query_w)

time: 295 us -> 279 us (0.946)
  waiting for transfers between devices: 156 us -> 140 us
    psum x1 -> x0, waiting for transfers between devices: 45.9 us -> none  [per_device(): enc_total = lax.psum(product(enc_agg, enc_out_w), 'mp')]
    all_gather x0 -> x1, waiting for transfers between devices: none -> 29.3 us  [per_device(): lax.all_gather(product(enc_agg, enc_out_w), 'mp')]
  transfers between devices with their start and end apart: 6 -> 6, of which waited for: 4 -> 4; matrix products, arithmetic and copies ran while one was open for 10% -> 11% of each run, Pallas kernels for 0% -> 0%
where the time goes in v1:
time: 279 us; the launch traced here: 278 us
  waiting for transfers between devices  140 us (50%)
  local copies, waits for them, and re-layouts  72.5 us (26%)
  matrix products  36.4 us (13%)
  between operations  13.6 us (5%)
  other arithmetic  13.2 us (5%)
    reduce_scatter x1, waiting for transfers between devices, per_device(): lax.psum_scatter(product(dec_agg, dec_out_w), 'mp', scatter_dimension=1,...  53 us
    psum x1, waiting for transfers between devices, per_device(): lax.psum(product(attended, out_w) + product(hidden, down_w), 'mp')  41.8 us
    gather x2, local copies, waits for them, and re-layouts, edge_pass(): target_side[target]  35.2 us
    gather x2, local copies, waits for them, and re-layouts, edge_pass(): source_side[source] + target_side[target]  35.2 us
    all_gather x1, waiting for transfers between devices, per_device(): lax.all_gather(product(enc_agg, enc_out_w), 'mp')  29.3 us
    dot_general x12, matrix products, product(): jnp.dot(matrix, weight, precision=FULL_PRECISION, preferred_element_type=...  22.7 us
    all_gather x1, waiting for transfers between devices, per_device(): key_piece = lax.all_gather(key_values, 'nodes', axis=0, tiled=True)  15.6 us
  transfers between devices with their start and end apart: 6, of which 4 were waited for; matrix products, arithmetic and copies ran while one was open for 11% of the time, Pallas kernels for 0%

profile of v1, /device:TPU:0, one launch (start us, length us, event | category | flops | bytes accessed | tf_op | source)
XLA Modules:
  0.0 278.1 jit_solution(11596507774854416266)
XLA Ops:
  8.9 1.4 fusion.81
  10.4 5.2 %fusion.80 = f32[2048,128]{1,0:T(8,128)S(1)} fusion(f32[2048,512]{1,0:T(8,128)} %param.21, f32[512,128]{1,0:T(8,128)} %param.23), kind=kOutput, calls=%fused_computation.122 | convolution fusion | flops 1610612736 | bytes 5505024 | tf_op jit(solution)/shard_map/dot_general | solution.py:26
  15.7 14.2 %gather_fusion = f32[4096,128]{1,0:T(8,128)} fusion(f32[2048,128]{1,0:T(8,128)S(1)} %fusion.80, s32[4096]{0:T(1024)S(1)} %get-tuple-element.20), kind=kCustom, calls=%fused_computation | custom fusion | bytes 4210688 | tf_op jit(solution)/shard_map/gather | solution.py:41
  29.9 14.2 %gather_fusion.1 = f32[4096,128]{1,0:T(8,128)} fusion(f32[128,128]{1,0:T(8,128)S(1)} %fusion.81, s32[4096]{0:T(1024)S(1)} %get-tuple-element.21), kind=kCustom, calls=%fused_computation.1 | custom fusion | bytes 4210688 | tf_op jit(solution)/shard_map/gather | solution.py:41
  44.0 1.8 add.223
  45.9 1.9 fusion.10
  47.9 2.0 fusion.8
  51.0 29.3 %all-gather.6.cloned.1.call-done = f32[512,512]{1,0:T(8,128)} async-done(((f32[128,512]{1,0:T(8,128)}), f32[512,512]{1,0:T(8,128)}) %all-gather.6.cloned.1.call-update) | async-done | bytes 1048592 | tf_op jit(solution)/shard_map/all_gather | solution.py:94
  80.3 1.3 reduce_sum.63
  85.1 5.3 %fusion.83 = f32[2048,128]{1,0:T(8,128)S(1)} fusion(f32[2048,512]{1,0:T(8,128)} %param.21, f32[512,128]{1,0:T(8,128)S(1)} %copy-done.10), kind=kOutput, calls=%fused_computation.125 | convolution fusion | flops 1610612736 | bytes 5505024 | tf_op jit(solution)/shard_map/dot_general | solution.py:26
  92.4 15.6 %all-gather.4.cloned.1.call-done = f32[1024,256]{0,1:T(8,128)} async-done(((f32[128,256]{0,1:T(8,128)}), f32[1024,256]{0,1:T(8,128)}) %all-gather.4.cloned.1.call-update) | async-done | bytes 1048592 | tf_op jit(solution)/shard_map/all_gather | solution.py:105
  108.0 2.1 fusion.78
  110.4 1.8 fusion.22
  112.2 1.1 convolution_add_fusion
  113.5 41.8 %all-reduce.2.cloned.1.call-done = f32[128,512]{1,0:T(8,128)} async-done(((f32[128,512]{1,0:T(8,128)}), f32[128,512]{1,0:T(8,128)}) %all-reduce.2.cloned.1.call-update) | async-done | bytes 262160 | tf_op jit(solution)/shard_map/psum | solution.py:127
  157.0 2.3 collective-permute-start.1
  159.5 21.1 %gather_fusion.3 = f32[6144,128]{1,0:T(8,128)} fusion(f32[2048,128]{1,0:T(8,128)S(1)} %fusion.83, s32[6144]{0:T(1024)S(1)} %get-tuple-element.23), kind=kCustom, calls=%fused_computation.3 | custom fusion | bytes 6316032 | tf_op jit(solution)/shard_map/gather | solution.py:41
  180.6 21.0 %gather_fusion.2 = f32[6144,128]{1,0:T(8,128)} fusion(f32[384,128]{1,0:T(8,128)S(1)} %pad_maximum_fusion, s32[6144]{0:T(1024)S(1)} %get-tuple-element.22), kind=kCustom, calls=%fused_computation.2 | custom fusion | bytes 6316032 | tf_op jit(solution)/shard_map/gather | solution.py:41
  201.6 3.2 %add.224 = f32[6144,128]{1,0:T(8,128)S(1)} add(f32[6144,128]{1,0:T(8,128)} %gather_fusion.2, f32[6144,128]{1,0:T(8,128)} %gather_fusion.3) | non-fusion elementwise | flops 786432 | bytes 9437184 | tf_op jit(solution)/shard_map/add | solution.py:41
  204.8 3.0 %fusion.2 = f32[48,128,128]{2,1,0:T(8,128)S(1)} fusion(f32[48,128,128]{2,1,0:T(8,128)S(1)} %bitcast.95, s32[48,128]{1,0:T(8,128)S(1)} %bitcast.100), kind=kOutput, calls=%fused_computation.6 | convolution fusion | flops 1211891712 | bytes 6316032 | tf_op jit(solution)/shard_map/tne,teh->tnh/dot_general | solution.py:45
  207.7 2.9 %fusion = f32[16,128,128]{2,0,1:T(8,128)S(1)} fusion(f32[48,128,128]{2,1,0:T(8,128)S(1)} %fusion.2, s32[48]{0:T(128)S(1)} %get-tuple-element.13), kind=kOutput, calls=%fused_computation.4 | convolution fusion | flops 150995712 | bytes 4194496 | tf_op jit(solution)/shard_map/bt,tnh->bnh/dot_general | solution.py:47
  211.0 4.9 %fusion.84 = f32[2048,512]{1,0:T(8,128)} fusion(f32[2048,128]{1,0:T(8,128)S(1)} %bitcast.94, f32[128,512]{1,0:T(8,128)S(1)} %copy-done.11), kind=kOutput, calls=%fused_computation.126 | convolution fusion | flops 1610612736 | bytes 5505024 | tf_op jit(solution)/shard_map/dot_general | solution.py:26
  216.0 53.0 %reduce-scatter.2.cloned.1.call-done = f32[2048,128]{1,0:T(8,128)} async-done(((f32[2048,512]{1,0:T(8,128)}), f32[2048,128]{1,0:T(8,128)}) %reduce-scatter.2.cloned.1.call-update) | async-done | bytes 1048592 | tf_op jit(solution)/shard_map/reduce_scatter | solution.py:140
  269.0 2.6 dynamic-slice_add_fusion
  (76 shorter events, 11.4 us)
Async XLA Ops:
  6.5 84.3 %copy-start = (f32[512,512]{1,0:T(8,128)S(1)}, f32[512,512]{1,0:T(8,128)}, u32[]{:S(2)}) copy-start(f32[512,512]{1,0:T(8,128)} %param.31) | copy-start | bytes 3145732
  6.5 73.8 %all-gather.6.cloned.1.call-start = ((), (), s32[]{:S(2)}) async-start(), calls=%async_computation.4 | async-start | bytes 1310720 | tf_op jit(solution)/shard_map/all_gather | solution.py:94
  29.9 14.2 %copy-start.1 = (f32[4096,128]{1,0:T(8,128)S(1)}, f32[4096,128]{1,0:T(8,128)}, u32[]{:S(2)}) copy-start(f32[4096,128]{1,0:T(8,128)} %gather_fusion) | copy-start | bytes 6291460
  45.8 1.9 copy-start.14
  45.9 4.0 %copy-start.4 = (f32[128,512]{1,0:T(8,128)S(1)}, f32[128,512]{1,0:T(8,128)}, u32[]{:S(2)}) copy-start(f32[128,512]{1,0:T(8,128)} %param.25) | copy-start | bytes 786436
  47.8 33.8 %copy-start.3 = (f32[128,512]{1,0:T(8,128)S(1)}, f32[128,512]{1,0:T(8,128)}, u32[]{:S(2)}) copy-start(f32[128,512]{1,0:T(8,128)} %param.22) | copy-start | bytes 786436
  47.8 34.2 %copy-start.5 = (f32[512,128]{1,0:T(8,128)S(1)}, f32[512,128]{1,0:T(8,128)}, u32[]{:S(2)}) copy-start(f32[512,128]{1,0:T(8,128)} %param.29) | copy-start | bytes 786436
  47.8 34.2 %copy-start.13 = (f32[512]{0:T(512)S(1)}, f32[512]{0:T(512)}, u32[]{:S(2)}) copy-start(f32[512]{0:T(512)} %param.26) | copy-start | bytes 6148
  47.8 34.8 %copy-start.6 = (f32[512,128]{1,0:T(8,128)S(1)}, f32[512,128]{1,0:T(8,128)}, u32[]{:S(2)}) copy-start(f32[512,128]{1,0:T(8,128)} %param.28) | copy-start | bytes 786436
  47.8 37.2 %copy-start.10 = (f32[512,128]{1,0:T(8,128)S(1)}, f32[512,128]{1,0:T(8,128)}, u32[]{:S(2)}) copy-start(f32[512,128]{1,0:T(8,128)} %param.34) | copy-start | bytes 786436
  50.9 57.1 %all-gather.4.cloned.1.call-start = ((), (), s32[]{:S(2)}) async-start(), calls=%async_computation.1 | async-start | bytes 1179648 | tf_op jit(solution)/shard_map/all_gather | solution.py:105
  82.6 7.7 %copy-start.7 = (f32[512,128]{1,0:T(8,128)S(1)}, f32[512,128]{1,0:T(8,128)}, u32[]{:S(2)}) copy-start(f32[512,128]{1,0:T(8,128)} %param.27) | copy-start | bytes 786436
  84.0 71.3 %all-reduce.2.cloned.1.call-start = ((), (), s32[]{:S(2)}) async-start(), calls=%async_computation.2 | async-start | bytes 524288 | tf_op jit(solution)/shard_map/psum | solution.py:127
  85.0 6.6 %copy-start.2 = (f32[512,512]{1,0:T(8,128)S(1)}, f32[512,512]{1,0:T(8,128)}, u32[]{:S(2)}) copy-start(f32[512,512]{1,0:T(8,128)} %param.32) | copy-start | bytes 3145732
  90.4 21.8 %copy-start.8 = (f32[128,512]{1,0:T(8,128)S(1)}, f32[128,512]{1,0:T(8,128)}, u32[]{:S(2)}) copy-start(f32[128,512]{1,0:T(8,128)} %param.30) | copy-start | bytes 786436
  90.8 22.6 %copy-start.16 = (s32[48,2]{0,1:T(2,128)S(1)}, s32[48,2]{0,1:T(2,128)}, u32[]{:S(2)}) copy-start(s32[48,2]{0,1:T(2,128)} %param.40) | copy-start | bytes 1156
  90.9 22.6 %copy-start.12 = (s32[48,2,128]{2,1,0:T(2,128)S(1)}, s32[48,2,128]{2,1,0:T(2,128)}, u32[]{:S(2)}) copy-start(s32[48,2,128]{2,1,0:T(2,128)} %param.41) | copy-start | bytes 147460
  91.6 65.0 %copy-start.9 = (f32[512,128]{1,0:T(8,128)S(1)}, f32[512,128]{1,0:T(8,128)}, u32[]{:S(2)}) copy-start(f32[512,128]{1,0:T(8,128)} %param.35) | copy-start | bytes 786436
  91.6 65.0 %copy-start.15 = (f32[512]{0:T(512)S(1)}, f32[512]{0:T(512)}, u32[]{:S(2)}) copy-start(f32[512]{0:T(512)} %param.33) | copy-start | bytes 6148
  113.3 155.6 %reduce-scatter.2.cloned.1.call-start = ((), (), s32[]{:S(2)}) async-start(), calls=%async_computation.3 | async-start | bytes 5242880 | tf_op jit(solution)/shard_map/reduce_scatter | solution.py:140
  157.0 23.5 %collective-permute-start.1 = (f32[128,128]{1,0:T(8,128)S(1)}, f32[128,128]{1,0:T(8,128)S(1)}, u32[]{:S(2)}, u32[]{:S(2)}) collective-permute-start(f32[128,128]{1,0:T(8,128)S(1)} %fusion.31), channel_id=1, source_target_pairs={{1,0},{2,1},{3,2},{4,3},{5,4},{6,5},{7,6},{0,7},{9,8},{10,9},{11,1... | collective-permute-start | bytes 196616 | tf_op jit(solution)/shard_map/ppermute | solution.py:20
  159.4 21.2 %collective-permute-start = (f32[128,128]{1,0:T(8,128)S(1)}, f32[128,128]{1,0:T(8,128)S(1)}, u32[]{:S(2)}, u32[]{:S(2)}) collective-permute-start(f32[128,128]{1,0:T(8,128)S(1)} %fusion.31), channel_id=1, source_target_pairs={{0,1},{1,2},{2,3},{3,4},{4,5},{5,6},{6,7},{7,0},{8,9},{9,10},{10,1... | collective-permute-start | bytes 196616 | tf_op jit(solution)/shard_map/ppermute | solution.py:19
  207.7 3.3 %copy-start.11 = (f32[128,512]{1,0:T(8,128)S(1)}, f32[128,512]{1,0:T(8,128)}, u32[]{:S(2)}) copy-start(f32[128,512]{1,0:T(8,128)} %param.36) | copy-start | bytes 786436
Sparse Core Ops, SparseCore 0:
  51.0 29.2 all-gather.5
  84.1 23.8 all-gather.3
  113.5 41.8 all-reduce.1
  216.1 52.8 reduce-scatter.1
